TPU v7x, 32 devices: a whole 2x2x4 slice. The times are simulated.
32 devices in a mesh: gx: 4 (over x, core), gy: 8 (over z, y).
Axes of the slice: x: 2, y: 2, z: 4, core: 2. Of those that a mesh axis runs over, the one named last changes fastest.
Arguments:
- velocity: float32 [3, 1024, 512], P(None, ('gx', 'gy')), may hold values from -6 to 6
- depart: float32 [3, 524288], P(None, ('gx', 'gy')), may hold values from -1 to 1
- owner_rank: int32 [524288, 1], P(('gx', 'gy')), may hold values from 0 to 31; in each aligned block of 16384 rows (0 to 16383, 16384 to 32767, ...) at most 1024 rows name the same one
- owner_element_index: int32 [524288], P(('gx', 'gy')), may hold values from 0 to 31
- neighbours: int32 [6, 1024], P(None, ('gx', 'gy')), may hold values from -1 to 1023, as said below
Outputs:
- advected: float32 [3, 1024, 512], P(None, ('gx', 'gy'))
Inputs may be any that keep to these rules, and one draw needn't show every extreme that they name: `owner_rank`: within the rows of one device no owner device is named by more than 1024 rows, and in some device's rows one owner is named exactly 1024 times. `neighbours`: -1 marks a boundary face; any other entry is an element of the same block of 32 consecutive elements as the entry's own element, or of the block just before or just after it.
All inputs are finite; a program needn't handle non-finite values.
Results may differ from a plain program's by a relative error of at most 0.0003.
Values sent between devices are 32-bit elements; how exact they have to be, the bound alone decides.
No kernel may reach another device: no remote copies, remote signals or barrier semaphores. Data moves between devices by JAX's collectives and lax.ppermute only.
A program may use at most 64 MiB of HBM per device.

v0:
```python
import math

import jax
import jax.numpy as jnp
import numpy as np
from jax import lax
from jax.sharding import PartitionSpec as P

GLL_POINTS = np.array(
    [
        -1.0,
        -0.8717401485096066,
        -0.5917001814331423,
        -0.2092992179024789,
        0.2092992179024789,
        0.5917001814331423,
        0.8717401485096066,
        1.0,
    ]
)


def with_halo(cells, sides, width):
    for axis, dim in sides:
        count = lax.axis_size(axis)
        ends = count - 1
        head = lax.slice_in_dim(cells, 0, width, axis=dim)
        tail = lax.slice_in_dim(cells, cells.shape[dim] - width, cells.shape[dim], axis=dim)
        cells = jnp.concatenate(
            [
                lax.ppermute(tail, axis, [(i, (i + 1) % count) for i in range(ends)]),
                cells,
                lax.ppermute(head, axis, [((i + 1) % count, i) for i in range(ends)]),
            ],
            axis=dim,
        )
    return cells


def lagrange(coords):
    columns = []
    for node_id in range(8):
        factor = jnp.ones_like(coords)
        for other in range(8):
            if other != node_id:
                factor = factor * (
                    (coords - float(GLL_POINTS[other]))
                    / float(GLL_POINTS[node_id] - GLL_POINTS[other])
                )
        columns.append(factor)
    return jnp.stack(columns, axis=-1)


def face_slicer(face_id):
    whole_range = slice(None)
    edge_at = 7 * (face_id % 2)
    if face_id < 2:
        return (whole_range, whole_range, edge_at)
    if face_id < 4:
        return (whole_range, whole_range, whole_range, edge_at)
    return (whole_range, whole_range, whole_range, whole_range, edge_at)


def faces_of(nodal_cube):
    shape_lead = (nodal_cube.shape[0], nodal_cube.shape[1], 64)
    return jnp.stack(
        [nodal_cube[face_slicer(face_id)].reshape(shape_lead) for face_id in range(6)], axis=1
    )


def apply_faces_hot(nodal_cube, own_faces, neighbour_faces, local_index, present):
    result = nodal_cube
    extended_count = neighbour_faces.shape[2]
    columns = jnp.arange(extended_count, dtype=jnp.int32)
    for face_id in range(6):
        picker = (local_index[face_id][:, None] == columns[None, :]).astype(jnp.float32)
        across_elements = jnp.einsum(
            "em,cmq->ceq", picker, neighbour_faces[:, face_id ^ 1], precision=lax.Precision.HIGHEST
        )
        change = jnp.where(
            present[face_id][None, :, None], 0.5 * (across_elements - own_faces[:, face_id]), 0.0
        )
        result = result.at[face_slicer(face_id)].add(
            change.reshape(result.shape[0], result.shape[1], 8, 8)
        )
    return result


def bucket_slots(owners, peer_count):
    points = owners.shape[0]
    step_size = math.gcd(points, 2048)
    sub_blocks = step_size // 128
    row_ids = lax.broadcasted_iota(jnp.int32, (128, 128), 0)
    col_ids = lax.broadcasted_iota(jnp.int32, (128, 128), 1)
    lower_triangle = (col_ids < row_ids).astype(jnp.bfloat16)
    targets = jnp.arange(peer_count, dtype=jnp.int32)

    def advance(running, step_owners):
        matches = step_owners.reshape(sub_blocks, 128)[:, :, None] == targets
        one_hot_mask = matches.astype(jnp.bfloat16)
        earlier_entries = jnp.einsum(
            "zw,lwn->lzn", lower_triangle, one_hot_mask, preferred_element_type=jnp.float32
        )
        totals = jnp.sum(one_hot_mask, axis=1, dtype=jnp.float32)
        before = jnp.cumsum(totals, axis=0) - totals + running[None, :]
        position = jnp.sum(jnp.where(matches, earlier_entries + before[:, None, :], 0.0), axis=2)
        return (running + jnp.sum(totals, axis=0), position.reshape(step_size).astype(jnp.int32))

    finished, bucket_slot = lax.scan(
        advance,
        jnp.zeros((peer_count,), jnp.float32),
        owners.reshape(points // step_size, step_size),
    )
    return bucket_slot.reshape(points)


def place_points(payload, owners, bucket_slot, peer_count, capacity):
    channels = payload.shape[0]
    points = owners.shape[0]
    block_size = math.gcd(points, 1024)
    block_count = points // block_size
    peer_ids = jnp.arange(peer_count, dtype=jnp.int32)
    slot_ids = jnp.arange(capacity, dtype=jnp.int32)

    def add_block(placed, block_triple):
        values, block_owners, block_slots = block_triple
        peer_hot = (block_owners[:, None] == peer_ids[None, :]).astype(jnp.float32)
        slot_hot = (block_slots[:, None] == slot_ids[None, :]).astype(jnp.float32)
        spread = values[:, :, None] * peer_hot[None]
        return (
            placed + jnp.einsum("cnp,ns->cps", spread, slot_hot, precision=lax.Precision.HIGHEST),
            None,
        )

    blocks = (
        payload.reshape(channels, block_count, block_size).transpose(1, 0, 2),
        owners.reshape(block_count, block_size),
        bucket_slot.reshape(block_count, block_size),
    )
    placed, unused = lax.scan(
        add_block, jnp.zeros((channels, peer_count, capacity), jnp.float32), blocks
    )
    return placed


def pick_answers(answers, owners, bucket_slot):
    channels, peer_count, capacity = answers.shape
    points = owners.shape[0]
    block_size = math.gcd(points, 1024)
    block_count = points // block_size
    peer_ids = jnp.arange(peer_count, dtype=jnp.int32)
    slot_ids = jnp.arange(capacity, dtype=jnp.int32)

    def one_block(block_pair):
        block_owners, block_slots = block_pair
        peer_hot = (block_owners[:, None] == peer_ids[None, :]).astype(jnp.float32)
        slot_hot = (block_slots[:, None] == slot_ids[None, :]).astype(jnp.float32)
        picked = jnp.einsum("cps,ns->cnp", answers, slot_hot, precision=lax.Precision.HIGHEST)
        return jnp.sum(picked * peer_hot[None], axis=2)

    values = lax.map(
        one_block,
        (owners.reshape(block_count, block_size), bucket_slot.reshape(block_count, block_size)),
    )
    return values.transpose(1, 0, 2).reshape(channels, points)


def interp_block(block_pair, nodal_table):
    coords, elem_ids = block_pair
    block_size = coords.shape[1]
    elem_count = nodal_table.shape[1] // 4
    weights = lagrange(coords)
    one_hot_mask = (elem_ids[:, None] == jnp.arange(elem_count, dtype=jnp.int32)[None, :]).astype(
        jnp.float32
    )
    summed = jnp.zeros((block_size, nodal_table.shape[2]), jnp.float32)
    for half_id in range(2):
        scaled = (
            weights[2][:, 4 * half_id : 4 * half_id + 4, None] * one_hot_mask[:, None, :]
        ).reshape(block_size, 4 * elem_count)
        summed = summed + jnp.dot(
            scaled,
            nodal_table[half_id],
            precision=lax.Precision.HIGHEST,
            preferred_element_type=jnp.float32,
        )
    rs_plane = (weights[0][:, :, None] * weights[1][:, None, :]).reshape(block_size, 1, 64)
    values = jnp.sum(summed.reshape(block_size, nodal_table.shape[2] // 64, 64) * rs_plane, axis=2)
    return values.T


def interpolate(coords, elem_ids, nodal_table):
    peer_count = coords.shape[1]
    slots_each = coords.shape[2]
    point_total = peer_count * slots_each
    block_size = math.gcd(point_total, 4096)
    block_count = point_total // block_size
    coord_blocks = coords.reshape(3, block_count, block_size).transpose(1, 0, 2)
    element_blocks = elem_ids.reshape(block_count, block_size)
    values = lax.map(
        lambda block_pair: interp_block(block_pair, nodal_table), (coord_blocks, element_blocks)
    )
    return values.transpose(1, 0, 2).reshape(3, peer_count, slots_each)


def local(velocity, depart, owner_rank, owner_element_index, neighbours):
    outer_count = lax.axis_size("gx")
    inner_count = lax.axis_size("gy")
    peer_count = outer_count * inner_count
    elem_count = velocity.shape[1]
    points = depart.shape[1]
    capacity = 2 * points // peer_count
    owners = owner_rank[:, 0]
    bucket_slot = bucket_slots(owners, peer_count)
    payload = jnp.concatenate(
        [depart, (owner_element_index + 1).astype(jnp.float32)[None, :]], axis=0
    )
    placed = place_points(payload, owners, bucket_slot, peer_count, capacity)
    send_coords = placed[0:3]
    send_elems = (placed[3:4] - 1.0).astype(jnp.int32)
    nodal_table = (
        velocity.reshape(3, elem_count, 8, 8, 8)
        .transpose(4, 1, 0, 2, 3)
        .reshape(2, 4 * elem_count, 192)
    )
    answers = interpolate(
        lax.all_to_all(send_coords, ("gx", "gy"), split_axis=1, concat_axis=1, tiled=True),
        lax.all_to_all(send_elems, ("gx", "gy"), split_axis=1, concat_axis=1, tiled=True)[0],
        nodal_table,
    )
    answers = lax.all_to_all(answers, ("gx", "gy"), split_axis=1, concat_axis=1, tiled=True)
    departed = pick_answers(answers, owners, bucket_slot)
    nodal_cube = departed.reshape(3, elem_count, 8, 8, 8)
    own_faces = faces_of(nodal_cube)
    extended = with_halo(own_faces, ((("gx", "gy"), 2),), elem_count)
    device_id = lax.axis_index("gx") * inner_count + lax.axis_index("gy")
    first_elem = (device_id - 1) * elem_count
    present = neighbours >= 0
    local_index = jnp.where(present, neighbours - first_elem, 0)
    result = apply_faces_hot(nodal_cube, own_faces, extended, local_index, present)
    return result.reshape(3, elem_count, 512)


def solution(mesh):
    placed = (
        P(None, ("gx", "gy"), None),
        P(None, ("gx", "gy")),
        P(("gx", "gy"), None),
        P(("gx", "gy")),
        P(None, ("gx", "gy")),
    )
    return jax.shard_map(
        local, mesh=mesh, in_specs=placed, out_specs=P(None, ("gx", "gy"), None), check_vma=False
    )
```

profile of v0, /device:TPU:0, one launch (start us, length us, event | category | flops | bytes accessed | tf_op | source)
XLA Modules:
  0.0 390.5 jit_solution(15041983891645134162)
XLA Ops:
  2.2 5.9 %while.55 = (s32[]{:T(128)}, f32[32]{0:T(128)S(1)}, s32[8,2048]{1,0:T(8,128)S(1)}, s32[8,2048]{1,0:T(8,128)S(1)}, s32[]{:T(128)}, /*index=5*/s32[]{:T(128)}, f32[]{:T(128)}) while((s32[]{:T(128)}, f32[32]{0:T(128)S(1)}, s32[8,2048]{1,0:T(8,128)S(1)}, s32[8,2048]{1,0:T(8,128)S(1)}, s32[]{:T(128)}, /*index=5*/s32[]{:T(128)}, ...), condition=%wide.region_5.6_spmd.clone, body=%wide.region_0.5_spmd.clone.sunk | while | flops 17473572 | bytes 88939 | solution.py:109
  8.4 30.2 %while.56 = (s32[]{:T(128)}, f32[4,32,1024]{2,1,0:T(8,128)S(1)}, f32[16,4,1024]{2,1,0:T(4,128)S(1)}, s32[16,1024]{1,0:T(8,128)S(1)}, s32[16,1024]{1,0:T(8,128)S(1)}, /*index=5*/s32[]{:T(128)}, s32[]{:T(128)}) while((s32[]{:T(128)}, f32[4,32,1024]{2,1,0:T(8,128)S(1)}, f32[16,4,1024]{2,1,0:T(4,128)S(1)}, s32[16,1024]{1,0:T(8,128)S(1)}, ...), condition=%wide.region_7.8_spmd.clone, body=%wide.region_6.7_spmd.clone.sunk | while | flops 1612120064 | bytes 1384551 | solution.py:140
  39.4 7.3 %all-to-all-start.1 = ((s32[1,32,1024]{2,0,1:T(1,128)}), s32[1,32,1024]{2,0,1:T(1,128)S(1)}, u32[]{:S(2)}, u32[]{:S(2)}) async-start(s32[1,32,1024]{2,0,1:T(1,128)} %copy.152), calls=%async_computation.1 | async-start | bytes 262144 | tf_op jit(solution)/shard_map/all_to_all | solution.py:228
  47.9 6.7 %all-to-all-done.1 = s32[1,32,1024]{2,0,1:T(1,128)S(1)} async-done(((s32[1,32,1024]{2,0,1:T(1,128)}), s32[1,32,1024]{2,0,1:T(1,128)S(1)}, u32[]{:S(2)}, u32[]{:S(2)}) %all-to-all-start.1) | async-done | bytes 131104 | tf_op jit(solution)/shard_map/all_to_all | solution.py:228
  54.5 2.8 all-to-all-start
  58.4 14.9 %all-to-all-done = f32[3,32,1024]{2,0,1:T(4,128)S(1)} async-done(((f32[3,32,1024]{2,0,1:T(4,128)}), f32[3,32,1024]{2,0,1:T(4,128)S(1)}, u32[]{:S(2)}, u32[]{:S(2)}) %all-to-all-start) | async-done | bytes 393248 | tf_op jit(solution)/shard_map/all_to_all | solution.py:227
  73.8 75.3 %while.53 = (s32[]{:T(128)}, f32[8,3,4096]{2,1,0:T(4,128)}, f32[8,3,4096]{2,0,1:T(8,128)S(1)}, s32[8,4096]{1,0:T(8,128)S(1)}, f32[2,128,192]{2,1,0:T(8,128)S(1)}, /*index=5*/s32[]{:T(128)}) while((s32[]{:T(128)}, f32[8,3,4096]{2,1,0:T(4,128)}, f32[8,3,4096]{2,0,1:T(8,128)S(1)}, s32[8,4096]{1,0:T(8,128)S(1)}, f32[2,128,192]{2,1,0:T(8,128)S(1)}, ...), condition=%wide.region_10.11_spmd, body=%wide.region_8.10_spmd.sunk | while | flops 2421215232 | bytes 27263064 | solution.py:200
  79.3 2.8 convolution_add_fusion.3
  117.0 2.8 convolution_add_fusion.3
  149.1 2.8 all-to-all-start.2
  152.6 15.4 %all-to-all-done.2 = f32[3,32,1024]{2,0,1:T(4,128)S(1)} async-done(((f32[3,32,1024]{2,0,1:T(4,128)}), f32[3,32,1024]{2,0,1:T(4,128)S(1)}, u32[]{:S(2)}, u32[]{:S(2)}) %all-to-all-start.2) | async-done | bytes 393248 | tf_op jit(solution)/shard_map/all_to_all | solution.py:231
  168.2 38.9 %while.54 = (s32[]{:T(128)}, f32[16,3,1024]{2,1,0:T(4,128)S(1)}, s32[16,1024]{1,0:T(8,128)S(1)}, f32[3,32,1024]{2,1,0:T(8,128)S(1)}, s32[16,1024]{1,0:T(8,128)S(1)}, /*index=5*/s32[]{:T(128)}) while((s32[]{:T(128)}, f32[16,3,1024]{2,1,0:T(4,128)S(1)}, s32[16,1024]{1,0:T(8,128)S(1)}, f32[3,32,1024]{2,1,0:T(8,128)S(1)}, ...), condition=%wide.region_13.14_spmd.clone, body=%wide.region_11.13_spmd.clone.sunk | while | flops 1209267200 | bytes 725077 | solution.py:161
  211.1 3.7 fusion.87
  222.7 3.0 copy.161
  225.7 3.0 copy.162
  237.0 5.3 %collective-permute-start = (f32[3,6,32,64]{3,2,1,0:T(8,128)}, f32[3,6,32,64]{3,2,1,0:T(8,128)}, u32[]{:S(2)}, u32[]{:S(2)}) collective-permute-start(f32[3,6,32,64]{3,2,1,0:T(8,128)} %copy.163), channel_id=1, source_target_pairs={{0,1},{1,2},{2,3},{3,4},{4,5},{5,6},{6,7},{7,8},{8,9},{9,10},{10,1... | collective-permute-start | bytes 442376 | tf_op jit(solution)/shard_map/ppermute | solution.py:31
  269.8 8.2 %scatter-add.24 = f32[3,32,8,8,8]{4,3,2,1,0:T(8,128)S(1)} dynamic-update-slice(f32[3,32,8,8,8]{4,3,2,1,0:T(8,128)S(1)} %fusion.66, f32[3,32,8,1,8]{4,3,2,1,0:T(1,128)S(1)} %slice_add_fusion.3, s32[]{:T(128)} %constant.517.clone.1, s32[]{:T(128)} %constant.517.clone.1, s32[]{:T(128)} %constant.517.clone.1, s32[]{:T(128)} %constant.517.clone.1, s32[]{:T(128)} %constant.517.clone.1) | dynamic-update-slice | bytes 49156 | tf_op jit(solution)/shard_map/scatter-add | solution.py:83
  284.4 4.4 %copy.186 = f32[3,32,8,8,1]{4,3,2,1,0:T(8,128)} copy(f32[3,32,8,8,1]{1,3,2,0,4:T(8,128)} %bitcast.294) | data formatting | bytes 49152 | tf_op jit(solution)/shard_map/reshape.208
  290.1 9.1 %scatter-add.25 = f32[3,32,8,8,8]{4,3,2,1,0:T(8,128)S(1)} dynamic-update-slice(f32[3,32,8,8,8]{4,3,2,1,0:T(8,128)S(1)} %scatter-add.24, f32[3,32,8,1,8]{4,3,2,1,0:T(1,128)} %slice_add_fusion.2, s32[]{:T(128)} %constant.517.clone.1, s32[]{:T(128)} %constant.517.clone.1, s32[]{:T(128)} %constant.517.clone.1, s32[]{:T(128)} %constant.527.clone.1, s32[]{:T(128)} %constant.517.clone.1) | dynamic-update-slice | bytes 49156 | tf_op jit(solution)/shard_map/scatter-add | solution.py:83
  299.2 4.2 %slice_add_fusion.1 = f32[3,32,8,8,1]{4,3,2,1,0:T(8,128)} fusion(f32[3,32,8,8,1]{4,3,2,1,0:T(8,128)} %copy.186, f32[3,32,8,8,8]{4,3,2,1,0:T(8,128)S(1)} %scatter-add.25), kind=kLoop, calls=%fused_computation.80 | loop fusion | flops 6144 | bytes 73728 | tf_op jit(solution)/shard_map/add | solution.py:83
  303.4 10.8 %scatter-add.26 = f32[3,32,8,8,8]{4,3,2,1,0:T(8,128)S(1)} dynamic-update-slice(f32[3,32,8,8,8]{4,3,2,1,0:T(8,128)S(1)} %scatter-add.25, f32[3,32,8,8,1]{4,3,2,1,0:T(8,128)} %slice_add_fusion.1, s32[]{:T(128)} %constant.517.clone.1, s32[]{:T(128)} %constant.517.clone.1, s32[]{:T(128)} %constant.517.clone.1, s32[]{:T(128)} %constant.517.clone.1, s32[]{:T(128)} %constant.517.clone.1) | dynamic-update-slice | bytes 49156 | tf_op jit(solution)/shard_map/scatter-add | solution.py:83
  315.5 3.6 copy.190
  319.1 4.4 %slice_add_fusion = f32[3,32,8,8,1]{4,3,2,1,0:T(8,128)} fusion(f32[3,32,8,8,1]{4,3,2,1,0:T(8,128)} %copy.190, f32[3,32,8,8,8]{4,3,2,1,0:T(8,128)S(1)} %scatter-add.26), kind=kLoop, calls=%fused_computation.79 | loop fusion | flops 6144 | bytes 73728 | tf_op jit(solution)/shard_map/add | solution.py:83
  323.5 62.6 %scatter-add.29 = f32[3,32,8,8,8]{4,3,2,1,0:T(8,128)S(1)} dynamic-update-slice(f32[3,32,8,8,8]{4,3,2,1,0:T(8,128)S(1)} %scatter-add.26, f32[3,32,8,8,1]{4,3,2,1,0:T(8,128)} %slice_add_fusion, s32[]{:T(128)} %constant.517.clone.1, s32[]{:T(128)} %constant.517.clone.1, s32[]{:T(128)} %constant.517.clone.1, s32[]{:T(128)} %constant.517.clone.1, s32[]{:T(128)} %constant.527.clone.1) | dynamic-update-slice | bytes 49156 | tf_op jit(solution)/shard_map/scatter-add | solution.py:83
  (388 shorter events, 209.7 us)
Async XLA Ops:
  0.0 8.2 %copy-start.4 = (s32[16384,1]{0,1:T(1,128)S(1)}, s32[16384,1]{0,1:T(1,128)}, u32[]{:S(2)}) copy-start(s32[16384,1]{0,1:T(1,128)} %param.27) | copy-start | bytes 196612
  0.0 8.1 %copy-start.8 = (s32[16384]{0:T(1024)S(1)}, s32[16384]{0:T(1024)}, u32[]{:S(2)}) copy-start(s32[16384]{0:T(1024)} %param.28) | copy-start | bytes 196612
  0.0 8.2 %copy-start.3 = (f32[3,16384]{1,0:T(4,128)S(1)}, f32[3,16384]{1,0:T(4,128)}, u32[]{:S(2)}) copy-start(f32[3,16384]{1,0:T(4,128)} %param.26) | copy-start | bytes 589828
  8.3 49.0 %copy-start.7 = (f32[3,32,512]{2,1,0:T(8,128)S(1)}, f32[3,32,512]{2,1,0:T(8,128)}, u32[]{:S(2)}) copy-start(f32[3,32,512]{2,1,0:T(8,128)} %param.25) | copy-start | bytes 589828
  39.4 15.2 %all-to-all-start.1 = ((s32[1,32,1024]{2,0,1:T(1,128)}), s32[1,32,1024]{2,0,1:T(1,128)S(1)}, u32[]{:S(2)}, u32[]{:S(2)}) async-start(s32[1,32,1024]{2,0,1:T(1,128)} %copy.152), calls=%async_computation.1 | async-start | bytes 262144 | tf_op jit(solution)/shard_map/all_to_all | solution.py:228
  54.5 18.8 %all-to-all-start = ((f32[3,32,1024]{2,0,1:T(4,128)}), f32[3,32,1024]{2,0,1:T(4,128)S(1)}, u32[]{:S(2)}, u32[]{:S(2)}) async-start(f32[3,32,1024]{2,0,1:T(4,128)} %bitcast.225), calls=%async_computation | async-start | bytes 1048576 | tf_op jit(solution)/shard_map/all_to_all | solution.py:227
  73.8 78.2 %copy-start.9 = (s32[6,32]{1,0:T(8,128)S(1)}, s32[6,32]{1,0:T(8,128)}, u32[]{:S(2)}) copy-start(s32[6,32]{1,0:T(8,128)} %param.29) | copy-start | bytes 2308
  149.1 18.8 %all-to-all-start.2 = ((f32[3,32,1024]{2,0,1:T(4,128)}), f32[3,32,1024]{2,0,1:T(4,128)S(1)}, u32[]{:S(2)}, u32[]{:S(2)}) async-start(f32[3,32,1024]{2,0,1:T(4,128)} %bitcast.27), calls=%async_computation.2 | async-start | bytes 1048576 | tf_op jit(solution)/shard_map/all_to_all | solution.py:231
  222.7 6.0 %copy-start.2 = (f32[3,32,1,8,8]{1,4,3,0,2:T(8,128)S(1)}, f32[3,32,1,8,8]{1,4,3,0,2:T(8,128)}, u32[]{:S(2)}) copy-start(f32[3,32,1,8,8]{1,4,3,0,2:T(8,128)} %copy.158) | copy-start | bytes 73732
  225.7 17.2 %copy-start.1 = (f32[3,32,1,8,8]{1,4,3,0,2:T(8,128)S(1)}, f32[3,32,1,8,8]{1,4,3,0,2:T(8,128)}, u32[]{:S(2)}) copy-start(f32[3,32,1,8,8]{1,4,3,0,2:T(8,128)} %copy.157) | copy-start | bytes 73732
  235.7 13.2 %collective-permute-start.1 = (f32[3,6,32,64]{3,2,1,0:T(8,128)}, f32[3,6,32,64]{3,2,1,0:T(8,128)}, u32[]{:S(2)}, u32[]{:S(2)}) collective-permute-start(f32[3,6,32,64]{3,2,1,0:T(8,128)} %copy.163), channel_id=1, source_target_pairs={{1,0},{2,1},{3,2},{4,3},{5,4},{6,5},{7,6},{8,7},{9,8},{10,9},{11,1... | collective-permute-start | bytes 442376 | tf_op jit(solution)/shard_map/ppermute | solution.py:33
  237.0 15.6 %collective-permute-start = (f32[3,6,32,64]{3,2,1,0:T(8,128)}, f32[3,6,32,64]{3,2,1,0:T(8,128)}, u32[]{:S(2)}, u32[]{:S(2)}) collective-permute-start(f32[3,6,32,64]{3,2,1,0:T(8,128)} %copy.163), channel_id=1, source_target_pairs={{0,1},{1,2},{2,3},{3,4},{4,5},{5,6},{6,7},{7,8},{8,9},{9,10},{10,1... | collective-permute-start | bytes 442376 | tf_op jit(solution)/shard_map/ppermute | solution.py:31
  243.6 13.6 %copy-start.6 = (f32[3,32,64]{2,1,0:T(8,128)S(1)}, f32[3,32,64]{2,1,0:T(8,128)}, u32[]{:S(2)}) copy-start(f32[3,32,64]{2,1,0:T(8,128)} %copy.168) | copy-start | bytes 73732
  243.6 13.6 %copy-start.12 = (pred[32]{0:T(512)(128)(4,1)S(1)}, pred[32]{0:T(512)(128)(4,1)}, u32[]{:S(2)}) copy-start(pred[32]{0:T(512)(128)(4,1)} %get-tuple-element.426) | copy-start | bytes 100
  251.0 12.2 %copy-start.10 = (s32[32]{0:T(128)S(1)}, s32[32]{0:T(128)}, u32[]{:S(2)}) copy-start(s32[32]{0:T(128)} %get-tuple-element.418) | copy-start | bytes 388
  256.4 0.8 copy-start
  303.4 10.8 %copy-start.5 = (f32[3,32,64]{2,1,0:T(8,128)S(1)}, f32[3,32,64]{2,1,0:T(8,128)}, u32[]{:S(2)}) copy-start(f32[3,32,64]{2,1,0:T(8,128)} %copy.188) | copy-start | bytes 73732
  303.4 10.8 %copy-start.11 = (pred[32]{0:T(512)(128)(4,1)S(1)}, pred[32]{0:T(512)(128)(4,1)}, u32[]{:S(2)}) copy-start(pred[32]{0:T(512)(128)(4,1)} %get-tuple-element.421) | copy-start | bytes 100
where the time goes:
time: 393 us; the launch traced here: 391 us
  local copies, waits for them, and re-layouts  172 us (44%)
  matrix products  120 us (31%)
  waiting for transfers between devices  38.6 us (10%)
  other arithmetic  37.5 us (10%)
  starting transfers between devices  19.5 us (5%)
    scatter-add x5, local copies, waits for them, and re-layouts, apply_faces_hot(): result.at[face_slicer(face_id)]  93 us
    dot_general x16, matrix products, interp_block(): jnp.dot(scaled, nodal_table[half_id], precision=lax.Precision.HIGHEST, pr...  44 us
    dot_general x16, matrix products, one_block(): jnp.einsum('cps,ns->cnp', answers, slot_hot, precision=lax.Precision.HIGH...  37.5 us
    dot_general x16, matrix products, add_block(): jnp.einsum('cnp,ns->cps', spread, slot_hot, precision=lax.Precision.HIGHEST)  28.8 us
    slice x8, local copies, waits for them, and re-layouts, faces_of(): nodal_cube[face_slicer(face_id)].reshape(shape_lead)  16.5 us
    all_to_all x1, waiting for transfers between devices, local(): lax.all_to_all(answers, ('gx', 'gy'), split_axis=1, concat_axis=1, tiled=...  15.4 us
    all_to_all x1, waiting for transfers between devices, local(): lax.all_to_all(send_coords, ('gx', 'gy'), split_axis=1, concat_axis=1, ti...  14.9 us
    another operation x7, local copies, waits for them, and re-layouts  14.9 us
  transfers between devices with their start and end apart: 5, of which 4 were waited for; matrix products, arithmetic and copies ran while one was open for 3% of the time, Pallas kernels for 0%

commit v1 on v0

v1 whole, which is shorter than its diff:
```python
import functools
import math

import jax
import jax.numpy as jnp
import numpy as np
from jax import lax
from jax.experimental import pallas as pl
from jax.experimental.pallas import tpu as pltpu
from jax.sharding import PartitionSpec as P

GLL_POINTS = np.array(
    [
        -1.0,
        -0.8717401485096066,
        -0.5917001814331423,
        -0.2092992179024789,
        0.2092992179024789,
        0.5917001814331423,
        0.8717401485096066,
        1.0,
    ]
)
ROW = 512
f32 = jnp.float32
bf16 = jnp.bfloat16


def split(values):
    head = values.astype(bf16)
    return head, (values - head.astype(f32)).astype(bf16)


def dot(lhs, rhs, dims):
    return lax.dot_general(lhs, rhs, (dims, ((), ())), preferred_element_type=f32)


def place_kernel(depart, owners, elems, placed, spots, acc, *, peers, width, rows_step):
    rows_all = placed.shape[1]
    capacity = rows_all // peers * width
    total = rows_step * ROW
    sub = 256
    before = lax.broadcasted_iota(jnp.int32, (sub, sub), 0) < lax.broadcasted_iota(
        jnp.int32, (sub, sub), 1
    )
    before = jnp.where(before, 1.0, 0.0).astype(bf16)
    peer_ids = lax.broadcasted_iota(jnp.int32, (peers, sub), 0)
    bucket_ids = lax.broadcasted_iota(jnp.int32, (rows_all, total), 0)
    place_ids = lax.broadcasted_iota(jnp.int32, (width, total), 0)
    acc[...] = jnp.zeros_like(acc)

    def add_step(step, count):
        first = step * rows_step
        owner_rows = [owners[pl.ds(first + row, 1), :] for row in range(rows_step)]
        pieces = [
            owner[:, at * sub : (at + 1) * sub] for owner in owner_rows for at in range(ROW // sub)
        ]
        hots = [jnp.where(peer_ids == piece, 1.0, 0.0) for piece in pieces]
        ranks = dot(jnp.concatenate(hots, axis=0).astype(bf16), before, ((1,), (0,)))
        spot_rows = []
        for at, hot in enumerate(hots):
            rank = ranks[at * peers : (at + 1) * peers]
            slot = jnp.sum(hot * (rank + count), axis=0, keepdims=True)
            spot_rows.append(pieces[at] * capacity + slot.astype(jnp.int32))
            count = count + jnp.sum(hot, axis=1, keepdims=True)
        spot = jnp.concatenate(spot_rows, axis=1)
        for row in range(rows_step):
            spots[pl.ds(first + row, 1), :] = spot[:, row * ROW : (row + 1) * ROW]
        bucket = spot // width
        bucket_hot = bucket_ids == bucket
        place_hot = jnp.where(place_ids == spot - bucket * width, 1.0, 0.0).astype(bf16)
        heads, tails = [], []
        for axis in range(3):
            value = jnp.concatenate(
                [depart[axis, pl.ds(first + row, 1), :] for row in range(rows_step)], axis=1
            )
            head = value.astype(bf16).astype(f32)
            heads.append(head)
            tails.append(value - head)
        elem = jnp.concatenate(
            [elems[pl.ds(first + row, 1), :] for row in range(rows_step)], axis=1
        )
        spread = [
            jnp.where(bucket_hot, value, 0.0).astype(bf16)
            for value in heads + tails + [elem.astype(f32)]
        ]
        acc[...] += dot(jnp.concatenate(spread, axis=0), place_hot, ((1,), (1,)))
        return count

    lax.fori_loop(0, owners.shape[0] // rows_step, add_step, jnp.zeros((peers, 1), f32))
    for axis in range(3):
        placed[axis] = (
            acc[axis * rows_all : (axis + 1) * rows_all]
            + acc[(3 + axis) * rows_all : (4 + axis) * rows_all]
        )
    placed[3] = acc[6 * rows_all : 7 * rows_all]


STEP = 8


def place(depart, owners, elems, peers, width):
    rows = depart.shape[1]
    rows_all = 2 * rows * ROW // width
    return pl.pallas_call(
        functools.partial(
            place_kernel, peers=peers, width=width, rows_step=math.gcd(rows, STEP)
        ),
        out_shape=[
            jax.ShapeDtypeStruct((4, rows_all, width), f32),
            jax.ShapeDtypeStruct((rows, ROW), jnp.int32),
        ],
        scratch_shapes=[pltpu.VMEM((7 * rows_all, width), f32)],
    )(depart, owners, elems)


def basis(coord):
    nodes = lax.broadcasted_iota(jnp.int32, (8, 1), 0)
    scale = jnp.zeros((8, 1), f32)
    for i in range(8):
        gaps = [GLL_POINTS[i] - GLL_POINTS[m] for m in range(8) if m != i]
        scale = jnp.where(nodes == i, float(1.0 / np.prod(gaps)), scale)
    spread = jnp.broadcast_to(coord, (8, coord.shape[1]))
    product = jnp.broadcast_to(scale, spread.shape)
    for m in range(8):
        product = product * jnp.where(nodes == m, 1.0, spread - float(GLL_POINTS[m]))
    return product


def interp_kernel(received, table, answers, parts, *, elem_count):
    @pl.when(pl.program_id(0) == 0)
    def _():
        parts[...] = jnp.concatenate(split(table[...]), axis=0)

    width = received.shape[2]
    elem_ids = lax.broadcasted_iota(jnp.int32, (elem_count, width), 0).astype(f32)
    both = parts[...]
    half = both.shape[0] // 2
    for row in range(received.shape[1]):
        weights = [basis(received[axis, row : row + 1, :]) for axis in range(3)]
        hot = elem_ids == received[3, row : row + 1, :]
        head = weights[2].astype(bf16).astype(f32)
        tail = weights[2] - head
        scaled_head = jnp.concatenate(
            [jnp.where(hot, head[k : k + 1], 0.0).astype(bf16) for k in range(8)], axis=0
        )
        scaled_tail = jnp.concatenate(
            [jnp.where(hot, tail[k : k + 1], 0.0).astype(bf16) for k in range(8)], axis=0
        )
        main = dot(both, scaled_head, ((1,), (0,)))
        rest = dot(both[:half], scaled_tail, ((1,), (0,)))
        along = main[:half] + main[half:] + rest
        for c in range(3):
            summed = along[c * 64 : c * 64 + 8] * weights[0][0:1]
            for i in range(1, 8):
                at = c * 64 + i * 8
                summed = summed + along[at : at + 8] * weights[0][i : i + 1]
            answers[c, row : row + 1, :] = jnp.sum(summed * weights[1], axis=0, keepdims=True)


def interpolate(received, table, elem_count):
    rows_all, width = received.shape[1:]
    rows_step = 8
    return pl.pallas_call(
        functools.partial(interp_kernel, elem_count=elem_count),
        grid=(rows_all // rows_step,),
        in_specs=[
            pl.BlockSpec((4, rows_step, width), lambda i: (0, i, 0)),
            pl.BlockSpec(table.shape, lambda i: (0, 0)),
        ],
        out_specs=pl.BlockSpec((3, rows_step, width), lambda i: (0, i, 0)),
        out_shape=jax.ShapeDtypeStruct((3, rows_all, width), f32),
        scratch_shapes=[pltpu.VMEM((2 * table.shape[0], table.shape[1]), bf16)],
        compiler_params=pltpu.CompilerParams(dimension_semantics=("arbitrary",)),
    )(received, table)


def pick_kernel(answers, spots, departed, parts):
    rows_all, width = answers.shape[1:]

    @pl.when(pl.program_id(0) == 0)
    def _():
        for c in range(3):
            head, tail = split(answers[c])
            parts[c * rows_all : (c + 1) * rows_all] = head
            parts[(3 + c) * rows_all : (4 + c) * rows_all] = tail

    for row in range(spots.shape[0]):
        spot = spots[row : row + 1, :]
        bucket = spot // width
        place_at = spot - bucket * width
        bucket_hot = lax.broadcasted_iota(jnp.int32, (rows_all, ROW), 0) == bucket
        place_hot = lax.broadcasted_iota(jnp.int32, (width, ROW), 0) == place_at
        place_hot = jnp.where(place_hot, 1.0, 0.0).astype(bf16)
        picked = dot(parts[...], place_hot, ((1,), (0,)))
        for c in range(3):
            both = (
                picked[c * rows_all : (c + 1) * rows_all]
                + picked[(3 + c) * rows_all : (4 + c) * rows_all]
            )
            departed[c, row : row + 1, :] = jnp.sum(
                jnp.where(bucket_hot, both, 0.0), axis=0, keepdims=True
            )


def pick(answers, spots):
    rows_all, width = answers.shape[1:]
    rows = spots.shape[0]
    rows_step = math.gcd(rows, 8)
    return pl.pallas_call(
        pick_kernel,
        grid=(rows // rows_step,),
        in_specs=[
            pl.BlockSpec((3, rows_all, width), lambda i: (0, 0, 0)),
            pl.BlockSpec((rows_step, ROW), lambda i: (i, 0)),
        ],
        out_specs=pl.BlockSpec((3, rows_step, ROW), lambda i: (0, i, 0)),
        out_shape=jax.ShapeDtypeStruct((3, rows, ROW), f32),
        scratch_shapes=[pltpu.VMEM((6 * rows_all, width), bf16)],
        compiler_params=pltpu.CompilerParams(dimension_semantics=("arbitrary",)),
    )(answers, spots)


def faces_kernel(own, before, after, across, advected, stacked):
    elem_count, nodes = own.shape[1:]
    extended = 3 * elem_count
    lanes = lax.broadcasted_iota(jnp.int32, (1, nodes), 1)
    columns = lax.broadcasted_iota(jnp.int32, (elem_count, extended), 1)
    pickers = []
    kept = jnp.ones((elem_count, nodes), f32)
    edges = []
    for face in range(6):
        stride = (64, 8, 1)[face // 2]
        edge = (lanes // stride) % 8 == 7 * (face % 2)
        edges.append(edge)
        there = across[:, face : face + 1]
        pickers.append(jnp.where(columns == there, 0.5, 0.0).astype(bf16))
        kept = kept - jnp.where(jnp.logical_and(edge, there >= 0), 0.5, 0.0)
    picker = jnp.concatenate(pickers, axis=1)
    for c in range(3):
        values = jnp.concatenate([before[c], own[c], after[c]], axis=0)
        for face in range(6):
            jump = 7 * (64, 8, 1)[face // 2]
            turn = jump if face % 2 else nodes - jump
            moved = jnp.where(edges[face], pltpu.roll(values, turn, 1), 0.0)
            head, tail = split(moved)
            stacked[face * extended : (face + 1) * extended, :nodes] = head
            stacked[face * extended : (face + 1) * extended, nodes:] = tail
        added = dot(picker, stacked[...], ((1,), (0,)))
        advected[c] = own[c] * kept + added[:, :nodes] + added[:, nodes:]


def faces(own, before, after, across):
    elem_count, nodes = own.shape[1:]
    return pl.pallas_call(
        faces_kernel,
        out_shape=jax.ShapeDtypeStruct(own.shape, f32),
        scratch_shapes=[pltpu.VMEM((18 * elem_count, 2 * nodes), bf16)],
    )(own, before, after, across)


def local(velocity, depart, owner_rank, owner_element_index, neighbours):
    axes = ("gx", "gy")
    inner_count = lax.axis_size("gy")
    peers = lax.axis_size("gx") * inner_count
    elem_count = velocity.shape[1]
    points = depart.shape[1]
    capacity = 2 * points // peers
    width = math.gcd(capacity, ROW)
    rows = points // ROW
    placed, spots = place(
        depart.reshape(3, rows, ROW),
        owner_rank.reshape(rows, ROW),
        owner_element_index.reshape(rows, ROW),
        peers,
        width,
    )
    table = (
        velocity.reshape(3, elem_count, 64, 8).transpose(0, 2, 3, 1).reshape(192, 8 * elem_count)
    )
    received = lax.all_to_all(placed, axes, split_axis=1, concat_axis=1, tiled=True)
    answers = interpolate(received, table, elem_count)
    answers = lax.all_to_all(answers, axes, split_axis=1, concat_axis=1, tiled=True)
    departed = pick(answers, spots).reshape(3, elem_count, 512)
    ends = peers - 1
    before = lax.ppermute(departed, axes, [(i, i + 1) for i in range(ends)])
    after = lax.ppermute(departed, axes, [(i + 1, i) for i in range(ends)])
    device_id = lax.axis_index("gx") * inner_count + lax.axis_index("gy")
    first_elem = (device_id - 1) * elem_count
    across = jnp.where(neighbours >= 0, neighbours - first_elem, -1).T
    return faces(departed, before, after, across)


def solution(mesh):
    placed = (
        P(None, ("gx", "gy"), None),
        P(None, ("gx", "gy")),
        P(("gx", "gy"), None),
        P(("gx", "gy")),
        P(None, ("gx", "gy")),
    )
    return jax.shard_map(
        local, mesh=mesh, in_specs=placed, out_specs=P(None, ("gx", "gy"), None), check_vma=False
    )
```

time: 393 us -> 105 us (0.27)
  local copies, waits for them, and re-layouts: 172 us -> 12.4 us
  matrix products: 120 us -> 0 us
  Pallas kernels: 0 us -> 37.3 us
  other arithmetic: 37.5 us -> 1.39 us
  starting transfers between devices: 19.5 us -> 14 us
    dot_general x62 -> x0, matrix products: 120 us -> none  [the longest x16 44 us: interp_block(): jnp.dot(scaled, nodal_table[half_id], precision=lax.Precision.HIGHEST, pr...]
    scatter-add x5 -> x0, local copies, waits for them, and re-layouts: 93 us -> none  [apply_faces_hot(): result.at[face_slicer(face_id)]]
    pallas_call x0 -> x4, Pallas kernels: none -> 37.3 us  [the longest x1 13.2 us: interpolate(): pl.pallas_call(functools.partial(interp_kernel, elem_count=elem_count), g...]
    another operation x28 -> x0, local copies, waits for them, and re-layouts: 30.5 us -> none
    slice x16 -> x0, local copies, waits for them, and re-layouts: 16.6 us -> none  [the longest x8 16.5 us: faces_of(): nodal_cube[face_slicer(face_id)].reshape(shape_lead)]
    mul x24 -> x0, other arithmetic: 16.3 us -> none  [the longest x8 11.8 us: lagrange(): factor * ((coords - float(GLL_POINTS[other])) / float(GLL_POINTS[node_id]...]
    add x20 -> x0, other arithmetic: 11.4 us -> none  [the longest x4 11.3 us: apply_faces_hot(): result.at[face_slicer(face_id)]]
    ppermute x2, waiting for transfers between devices: 1.67 us -> 8.95 us  [the longest x1 7.08 us: local(): before = lax.ppermute(departed, axes, [(i, i + 1) for i in range(ends)])]
  transfers between devices with their start and end apart: 5 -> 4, of which waited for: 4 -> 4; matrix products, arithmetic and copies ran while one was open for 3% -> 2% of each run, Pallas kernels for 0% -> 0%
where the time goes in v1:
time: 105 us
  waiting for transfers between devices  39.4 us (38%)
  Pallas kernels  37.3 us (36%)
  starting transfers between devices  14 us (13%)
  local copies, waits for them, and re-layouts  12.4 us (12%)
  other arithmetic  1.39 us (1%)
    all_to_all x1, waiting for transfers between devices, local(): lax.all_to_all(answers, axes, split_axis=1, concat_axis=1, tiled=True)  15.5 us
    all_to_all x1, waiting for transfers between devices, local(): lax.all_to_all(placed, axes, split_axis=1, concat_axis=1, tiled=True)  15 us
    pallas_call x1, Pallas kernels, interpolate(): pl.pallas_call(functools.partial(interp_kernel, elem_count=elem_count), g...  13.2 us
    pallas_call x1, Pallas kernels, place(): pl.pallas_call(functools.partial(place_kernel, peers=peers, width=width,...  11.3 us
    pallas_call x1, Pallas kernels, pick(): pl.pallas_call(pick_kernel, grid=(rows // rows_step,), in_specs=[pl.Block...  9.65 us
    all_to_all x1, starting transfers between devices, local(): lax.all_to_all(placed, axes, split_axis=1, concat_axis=1, tiled=True)  7.33 us
    ppermute x1, waiting for transfers between devices, local(): before = lax.ppermute(departed, axes, [(i, i + 1) for i in range(ends)])  7.08 us
    unnamed x16, local copies, waits for them, and re-layouts  4.17 us
  transfers between devices with their start and end apart: 4, of which 4 were waited for; matrix products, arithmetic and copies ran while one was open for 2% of the time, Pallas kernels for 0%

profile of v1, /device:TPU:0, one launch (start us, length us, event | category | flops | bytes accessed | tf_op | source)
XLA Modules:
  0.0 104.7 jit_solution(17190842934233500015)
XLA Ops:
  0.0 1.7 %copy.26 = f32[1,3,32,512]{3,2,1,0:T(8,128)} copy(f32[1,3,32,512]{3,1,2,0:T(4,128)} %bitcast.14) | data formatting | bytes 393216
  2.3 0.8 reduce.3
  3.1 0.6 reshape.16.owners
  3.9 0.6 reshape.17.elems
  4.5 11.3 %shard_map.55 = (f32[4,64,512]{2,1,0:T(8,128)}, s32[32,512]{1,0:T(8,128)}) custom-call(f32[3,32,512]{2,1,0:T(8,128)} %bitcast.13, s32[32,512]{1,0:T(8,128)} %reshape.16.owners, s32[32,512]{1,0:T(8,128)} %reshape.17.elems), custom_call_target="tpu_custom_call" | custom-call | tf_op jit(solution)/shard_map/pallas_call | solution.py:105
  15.9 2.2 %copy.14 = f32[4,64,512]{2,0,1:T(4,128)} copy(f32[4,64,512]{2,1,0:T(8,128)} %get-tuple-element.7) | data formatting | bytes 1048576 | tf_op jit(solution)/shard_map/pallas_call | solution.py:105
  18.0 7.3 %all-to-all-start = ((f32[4,64,512]{2,0,1:T(4,128)}), f32[4,64,512]{2,0,1:T(4,128)S(1)}, u32[]{:S(2)}, u32[]{:S(2)}) async-start(f32[4,64,512]{2,0,1:T(4,128)} %copy.14), calls=%async_computation | async-start | bytes 1048576 | tf_op jit(solution)/shard_map/all_to_all | solution.py:281
  25.6 0.9 reshape.20.table
  26.6 15.0 %all-to-all-done = f32[4,64,512]{2,0,1:T(4,128)S(1)} async-done(((f32[4,64,512]{2,0,1:T(4,128)}), f32[4,64,512]{2,0,1:T(4,128)S(1)}, u32[]{:S(2)}, u32[]{:S(2)}) %all-to-all-start) | async-done | bytes 524320 | tf_op jit(solution)/shard_map/all_to_all | solution.py:281
  41.6 1.0 copy.17.received
  42.6 13.2 %shard_map.56 = f32[3,64,512]{2,1,0:T(8,128)} custom-call(f32[4,64,512]{2,1,0:T(8,128)} %copy.17.received, f32[192,256]{1,0:T(8,128)} %reshape.20.table), custom_call_target="tpu_custom_call" | custom-call | tf_op jit(solution)/shard_map/pallas_call | solution.py:164
  55.8 2.1 %copy.19 = f32[3,64,512]{2,0,1:T(4,128)} copy(f32[3,64,512]{2,1,0:T(8,128)} %shard_map.56) | data formatting | bytes 786432 | tf_op jit(solution)/shard_map/pallas_call | solution.py:164
  57.8 2.6 %all-to-all-start.1 = ((f32[3,64,512]{2,0,1:T(4,128)}), f32[3,64,512]{2,0,1:T(4,128)S(1)}, u32[]{:S(2)}, u32[]{:S(2)}) async-start(f32[3,64,512]{2,0,1:T(4,128)} %copy.19), calls=%async_computation.1 | async-start | bytes 1048576 | tf_op jit(solution)/shard_map/all_to_all | solution.py:283
  60.5 0.7 copy-done.5
  61.2 15.5 %all-to-all-done.1 = f32[3,64,512]{2,0,1:T(4,128)S(1)} async-done(((f32[3,64,512]{2,0,1:T(4,128)}), f32[3,64,512]{2,0,1:T(4,128)S(1)}, u32[]{:S(2)}, u32[]{:S(2)}) %all-to-all-start.1) | async-done | bytes 393248 | tf_op jit(solution)/shard_map/all_to_all | solution.py:283
  76.7 0.9 copy.20.answers
  77.6 9.6 %shard_map.57.own = f32[3,32,512]{2,1,0:T(8,128)} custom-call(f32[3,64,512]{2,1,0:T(8,128)} %copy.20.answers, s32[32,512]{1,0:T(8,128)} %get-tuple-element.8.spots), custom_call_target="tpu_custom_call" | custom-call | tf_op jit(solution)/shard_map/pallas_call | solution.py:210
  87.2 2.8 %collective-permute-start = (f32[3,32,512]{2,1,0:T(8,128)}, f32[3,32,512]{2,1,0:T(8,128)S(1)}, u32[]{:S(2)}, u32[]{:S(2)}) collective-permute-start(f32[3,32,512]{2,1,0:T(8,128)} %shard_map.57.own), channel_id=1, source_target_pairs={{0,1},{1,2},{2,3},{3,4},{4,5},{5,6},{6,7},{7,8},{8,9},{9,10},{10,1... | collective-permute-start | bytes 589832 | tf_op jit(solution)/shard_map/ppermute | solution.py:286
  90.0 1.3 %collective-permute-start.1 = (f32[3,32,512]{2,1,0:T(8,128)}, f32[3,32,512]{2,1,0:T(8,128)S(1)}, u32[]{:S(2)}, u32[]{:S(2)}) collective-permute-start(f32[3,32,512]{2,1,0:T(8,128)} %shard_map.57.own), channel_id=1, source_target_pairs={{1,0},{2,1},{3,2},{4,3},{5,4},{6,5},{7,6},{8,7},{9,8},{10,9},{11,1... | collective-permute-start | bytes 589832 | tf_op jit(solution)/shard_map/ppermute | solution.py:287
  91.3 0.6 select_bitcast_fusion.across
  91.9 7.1 %collective-permute-done.before = f32[3,32,512]{2,1,0:T(8,128)S(1)} collective-permute-done((f32[3,32,512]{2,1,0:T(8,128)}, f32[3,32,512]{2,1,0:T(8,128)S(1)}, u32[]{:S(2)}, u32[]{:S(2)}) %collective-permute-start) | collective-permute-done | bytes 196640 | tf_op jit(solution)/shard_map/ppermute | solution.py:286
  99.0 1.9 %collective-permute-done.1.after = f32[3,32,512]{2,1,0:T(8,128)S(1)} collective-permute-done((f32[3,32,512]{2,1,0:T(8,128)}, f32[3,32,512]{2,1,0:T(8,128)S(1)}, u32[]{:S(2)}, u32[]{:S(2)}) %collective-permute-start.1) | collective-permute-done | bytes 196640 | tf_op jit(solution)/shard_map/ppermute | solution.py:287
  100.9 0.7 copy-done.1
  101.6 3.1 %shard_map.58 = f32[3,32,512]{2,1,0:T(8,128)} custom-call(f32[3,32,512]{2,1,0:T(8,128)} %shard_map.57.own, f32[3,32,512]{2,1,0:T(8,128)} %copy-done, f32[3,32,512]{2,1,0:T(8,128)} %copy-done.1, s32[32,6]{1,0:T(8,128)} %select_bitcast_fusion.across), custom_call_target="tpu_custom_call" | custom-call | tf_op jit(solution)/shard_map/pallas_call | solution.py:255
  (13 shorter events, 1.1 us)
Async XLA Ops:
  0.0 2.3 %copy-start.3 = (s32[16384,1]{0,1:T(1,128)S(1)}, s32[16384,1]{0,1:T(1,128)}, u32[]{:S(2)}) copy-start(s32[16384,1]{0,1:T(1,128)} %param.7) | copy-start | bytes 196612
  3.1 0.8 copy-start.4
  18.0 7.3 %copy-start.2 = (f32[3,32,512]{2,1,0:T(8,128)S(1)}, f32[3,32,512]{2,1,0:T(8,128)}, u32[]{:S(2)}) copy-start(f32[3,32,512]{2,1,0:T(8,128)} %param.5) | copy-start | bytes 589828
  18.0 23.6 %all-to-all-start = ((f32[4,64,512]{2,0,1:T(4,128)}), f32[4,64,512]{2,0,1:T(4,128)S(1)}, u32[]{:S(2)}, u32[]{:S(2)}) async-start(f32[4,64,512]{2,0,1:T(4,128)} %copy.14), calls=%async_computation | async-start | bytes 1048576 | tf_op jit(solution)/shard_map/all_to_all | solution.py:281
  57.8 18.8 %all-to-all-start.1 = ((f32[3,64,512]{2,0,1:T(4,128)}), f32[3,64,512]{2,0,1:T(4,128)S(1)}, u32[]{:S(2)}, u32[]{:S(2)}) async-start(f32[3,64,512]{2,0,1:T(4,128)} %copy.19), calls=%async_computation.1 | async-start | bytes 1048576 | tf_op jit(solution)/shard_map/all_to_all | solution.py:283
  60.5 0.7 copy-start.5
  87.2 11.8 %collective-permute-start = (f32[3,32,512]{2,1,0:T(8,128)}, f32[3,32,512]{2,1,0:T(8,128)S(1)}, u32[]{:S(2)}, u32[]{:S(2)}) collective-permute-start(f32[3,32,512]{2,1,0:T(8,128)} %shard_map.57.own), channel_id=1, source_target_pairs={{0,1},{1,2},{2,3},{3,4},{4,5},{5,6},{6,7},{7,8},{8,9},{9,10},{10,1... | collective-permute-start | bytes 589832 | tf_op jit(solution)/shard_map/ppermute | solution.py:286
  90.0 10.9 %collective-permute-start.1 = (f32[3,32,512]{2,1,0:T(8,128)}, f32[3,32,512]{2,1,0:T(8,128)S(1)}, u32[]{:S(2)}, u32[]{:S(2)}) collective-permute-start(f32[3,32,512]{2,1,0:T(8,128)} %shard_map.57.own), channel_id=1, source_target_pairs={{1,0},{2,1},{3,2},{4,3},{5,4},{6,5},{7,6},{8,7},{9,8},{10,9},{11,1... | collective-permute-start | bytes 589832 | tf_op jit(solution)/shard_map/ppermute | solution.py:287
  99.0 1.9 %copy-start = (f32[3,32,512]{2,1,0:T(8,128)}, f32[3,32,512]{2,1,0:T(8,128)S(1)}, u32[]{:S(2)}) copy-start(f32[3,32,512]{2,1,0:T(8,128)S(1)} %collective-permute-done.before) | copy-start | bytes 589828
  100.9 0.7 copy-start.1

commit v2 on v1

--- a/solution.py
+++ b/solution.py
@@ -1,4 +1,5 @@
 import functools
+import itertools
 import math
 
 import jax
@@ -36,8 +37,8 @@
 
 
 def place_kernel(depart, owners, elems, placed, spots, acc, *, peers, width, rows_step):
-    rows_all = placed.shape[1]
-    capacity = rows_all // peers * width
+    capacity = placed.shape[1] // 4 * width
+    rows_all = peers * capacity // width
     total = rows_step * ROW
     sub = 256
     before = lax.broadcasted_iota(jnp.int32, (sub, sub), 0) < lax.broadcasted_iota(
@@ -51,9 +52,11 @@
 
     def add_step(step, count):
         first = step * rows_step
-        owner_rows = [owners[pl.ds(first + row, 1), :] for row in range(rows_step)]
+        lines = total // 128
+        owner = owners[pl.ds(pl.multiple_of(step * lines, lines), lines), :]
         pieces = [
-            owner[:, at * sub : (at + 1) * sub] for owner in owner_rows for at in range(ROW // sub)
+            jnp.concatenate([owner[at : at + 1], owner[at + 1 : at + 2]], axis=1)
+            for at in range(0, lines, 2)
         ]
         hots = [jnp.where(peer_ids == piece, 1.0, 0.0) for piece in pieces]
         ranks = dot(jnp.concatenate(hots, axis=0).astype(bf16), before, ((1,), (0,)))
@@ -71,43 +74,44 @@
         place_hot = jnp.where(place_ids == spot - bucket * width, 1.0, 0.0).astype(bf16)
         heads, tails = [], []
         for axis in range(3):
-            value = jnp.concatenate(
-                [depart[axis, pl.ds(first + row, 1), :] for row in range(rows_step)], axis=1
-            )
+            value = depart[axis : axis + 1, pl.ds(pl.multiple_of(step * total, total), total)]
             head = value.astype(bf16).astype(f32)
             heads.append(head)
             tails.append(value - head)
-        elem = jnp.concatenate(
-            [elems[pl.ds(first + row, 1), :] for row in range(rows_step)], axis=1
-        )
+        elem = elems[pl.ds(pl.multiple_of(step * lines, lines), lines), :]
+        elem = jnp.concatenate([elem[at : at + 1] for at in range(lines)], axis=1)
         spread = [
             jnp.where(bucket_hot, value, 0.0).astype(bf16)
-            for value in heads + tails + [elem.astype(f32)]
+            for value in heads + [elem.astype(f32)] + tails
         ]
         acc[...] += dot(jnp.concatenate(spread, axis=0), place_hot, ((1,), (1,)))
         return count
 
-    lax.fori_loop(0, owners.shape[0] // rows_step, add_step, jnp.zeros((peers, 1), f32))
-    for axis in range(3):
-        placed[axis] = (
-            acc[axis * rows_all : (axis + 1) * rows_all]
-            + acc[(3 + axis) * rows_all : (4 + axis) * rows_all]
-        )
-    placed[3] = acc[6 * rows_all : 7 * rows_all]
+    steps = owners.shape[0] * 128 // total
+    lax.fori_loop(0, steps, add_step, jnp.zeros((peers, 1), f32))
+    each = capacity // width
+    for peer in range(peers):
+        for channel in range(4):
+            at = channel * rows_all + peer * each
+            value = acc[at : at + each, :]
+            if channel < 3:
+                value = value + acc[at + 4 * rows_all : at + 4 * rows_all + each, :]
+            placed[peer, channel * each : (channel + 1) * each, :] = value
 
 
 STEP = 8
 
 
 def place(depart, owners, elems, peers, width):
-    rows = depart.shape[1]
-    rows_all = 2 * rows * ROW // width
+    points = depart.shape[1]
+    rows = points // ROW
+    rows_all = 2 * points // width
     return pl.pallas_call(
         functools.partial(
             place_kernel, peers=peers, width=width, rows_step=math.gcd(rows, STEP)
         ),
         out_shape=[
-            jax.ShapeDtypeStruct((4, rows_all, width), f32),
+            jax.ShapeDtypeStruct((peers, 4 * rows_all // peers, width), f32),
             jax.ShapeDtypeStruct((rows, ROW), jnp.int32),
         ],
         scratch_shapes=[pltpu.VMEM((7 * rows_all, width), f32)],
@@ -136,9 +140,11 @@
     elem_ids = lax.broadcasted_iota(jnp.int32, (elem_count, width), 0).astype(f32)
     both = parts[...]
     half = both.shape[0] // 2
-    for row in range(received.shape[1]):
-        weights = [basis(received[axis, row : row + 1, :]) for axis in range(3)]
-        hot = elem_ids == received[3, row : row + 1, :]
+    each = received.shape[1] // 4
+    for peer, row in itertools.product(range(received.shape[0]), range(each)):
+        lines = [received[peer, c * each + row : c * each + row + 1, :] for c in range(4)]
+        weights = [basis(lines[axis]) for axis in range(3)]
+        hot = elem_ids == lines[3]
         head = weights[2].astype(bf16).astype(f32)
         tail = weights[2] - head
         scaled_head = jnp.concatenate(
@@ -155,35 +161,50 @@
             for i in range(1, 8):
                 at = c * 64 + i * 8
                 summed = summed + along[at : at + 8] * weights[0][i : i + 1]
-            answers[c, row : row + 1, :] = jnp.sum(summed * weights[1], axis=0, keepdims=True)
+            value = jnp.sum(summed * weights[1], axis=0, keepdims=True)
+            first = (c * each + row) * (width // 128)
+            for at in range(width // 128):
+                answers[peer, first + at : first + at + 1, :] = value[:, at * 128 : (at + 1) * 128]
 
 
 def interpolate(received, table, elem_count):
-    rows_all, width = received.shape[1:]
-    rows_step = 8
+    peers, channels, width = received.shape
+    each = channels // 4
+    peers_step = math.gcd(peers, max(1, 8 // each))
+    lines = 3 * each * width // 128
     return pl.pallas_call(
         functools.partial(interp_kernel, elem_count=elem_count),
-        grid=(rows_all // rows_step,),
+        grid=(peers // peers_step,),
         in_specs=[
-            pl.BlockSpec((4, rows_step, width), lambda i: (0, i, 0)),
+            pl.BlockSpec((peers_step, channels, width), lambda i: (i, 0, 0)),
             pl.BlockSpec(table.shape, lambda i: (0, 0)),
         ],
-        out_specs=pl.BlockSpec((3, rows_step, width), lambda i: (0, i, 0)),
-        out_shape=jax.ShapeDtypeStruct((3, rows_all, width), f32),
+        out_specs=pl.BlockSpec((peers_step, lines, 128), lambda i: (i, 0, 0)),
+        out_shape=jax.ShapeDtypeStruct((peers, lines, 128), f32),
         scratch_shapes=[pltpu.VMEM((2 * table.shape[0], table.shape[1]), bf16)],
         compiler_params=pltpu.CompilerParams(dimension_semantics=("arbitrary",)),
     )(received, table)
 
 
-def pick_kernel(answers, spots, departed, parts):
-    rows_all, width = answers.shape[1:]
+def pick_kernel(answers, spots, departed, gathered, parts):
+    width = parts.shape[1]
+    rows_all = parts.shape[0] // 6
+    each = rows_all // answers.shape[0]
+    pieces = width // 128
 
     @pl.when(pl.program_id(0) == 0)
     def _():
-        for c in range(3):
-            head, tail = split(answers[c])
-            parts[c * rows_all : (c + 1) * rows_all] = head
-            parts[(3 + c) * rows_all : (4 + c) * rows_all] = tail
+        for peer, c, row, at in itertools.product(
+            range(answers.shape[0]), range(3), range(each), range(pieces)
+        ):
+            line = (c * each + row) * pieces + at
+            into = c * rows_all + peer * each + row
+            gathered[into : into + 1, at * 128 : (at + 1) * 128] = answers[
+                peer, line : line + 1, :
+            ]
+        head, tail = split(gathered[...])
+        parts[: 3 * rows_all] = head
+        parts[3 * rows_all :] = tail
 
     for row in range(spots.shape[0]):
         spot = spots[row : row + 1, :]
@@ -203,20 +224,24 @@
             )
 
 
-def pick(answers, spots):
-    rows_all, width = answers.shape[1:]
+def pick(answers, spots, width):
+    peers, lines, _ = answers.shape
+    rows_all = peers * lines * 128 // (3 * width)
     rows = spots.shape[0]
     rows_step = math.gcd(rows, 8)
     return pl.pallas_call(
         pick_kernel,
         grid=(rows // rows_step,),
         in_specs=[
-            pl.BlockSpec((3, rows_all, width), lambda i: (0, 0, 0)),
+            pl.BlockSpec(answers.shape, lambda i: (0, 0, 0)),
             pl.BlockSpec((rows_step, ROW), lambda i: (i, 0)),
         ],
         out_specs=pl.BlockSpec((3, rows_step, ROW), lambda i: (0, i, 0)),
         out_shape=jax.ShapeDtypeStruct((3, rows, ROW), f32),
-        scratch_shapes=[pltpu.VMEM((6 * rows_all, width), bf16)],
+        scratch_shapes=[
+            pltpu.VMEM((3 * rows_all, width), f32),
+            pltpu.VMEM((6 * rows_all, width), bf16),
+        ],
         compiler_params=pltpu.CompilerParams(dimension_semantics=("arbitrary",)),
     )(answers, spots)
 
@@ -267,21 +292,20 @@
     points = depart.shape[1]
     capacity = 2 * points // peers
     width = math.gcd(capacity, ROW)
-    rows = points // ROW
     placed, spots = place(
-        depart.reshape(3, rows, ROW),
-        owner_rank.reshape(rows, ROW),
-        owner_element_index.reshape(rows, ROW),
+        depart,
+        owner_rank.reshape(points // 128, 128),
+        owner_element_index.reshape(points // 128, 128),
         peers,
         width,
     )
     table = (
         velocity.reshape(3, elem_count, 64, 8).transpose(0, 2, 3, 1).reshape(192, 8 * elem_count)
     )
-    received = lax.all_to_all(placed, axes, split_axis=1, concat_axis=1, tiled=True)
+    received = lax.all_to_all(placed, axes, split_axis=0, concat_axis=0, tiled=True)
     answers = interpolate(received, table, elem_count)
-    answers = lax.all_to_all(answers, axes, split_axis=1, concat_axis=1, tiled=True)
-    departed = pick(answers, spots).reshape(3, elem_count, 512)
+    answers = lax.all_to_all(answers, axes, split_axis=0, concat_axis=0, tiled=True)
+    departed = pick(answers, spots, width).reshape(3, elem_count, 512)
     ends = peers - 1
     before = lax.ppermute(departed, axes, [(i, i + 1) for i in range(ends)])
     after = lax.ppermute(departed, axes, [(i + 1, i) for i in range(ends)])

time: 105 us -> 93.8 us (0.89)
  local copies, waits for them, and re-layouts: 12.4 us -> 4.19 us
  waiting for transfers between devices: 39.4 us -> 36.6 us
    pallas_call x2 -> x0, local copies, waits for them, and re-layouts: 4.22 us -> none  [the longest x1 2.16 us: place(): pl.pallas_call(functools.partial(place_kernel, peers=peers, width=width,...]
    all_to_all x2, waiting for transfers between devices: 30.5 us -> 27.7 us  [the longest x1 15 us: local(): lax.all_to_all(placed, axes, split_axis=0, concat_axis=0, tiled=True)]
    all_to_all x2 -> x0, local copies, waits for them, and re-layouts: 1.82 us -> none  [the longest x1 0.95 us: local(): lax.all_to_all(placed, axes, split_axis=1, concat_axis=1, tiled=True)]
    reshape x2 -> x0, local copies, waits for them, and re-layouts: 1.26 us -> none  [the longest x1 0.63 us: local(): owner_rank.reshape(rows, ROW)]
    unnamed x16 -> x14, local copies, waits for them, and re-layouts: 4.17 us -> 3.26 us
where the time goes in v2:
time: 93.8 us; the launch traced here: 93.4 us
  Pallas kernels  37.9 us (40%)
  waiting for transfers between devices  36.6 us (39%)
  starting transfers between devices  14.1 us (15%)
  local copies, waits for them, and re-layouts  4.19 us (4%)
    all_to_all x1, waiting for transfers between devices, local(): lax.all_to_all(placed, axes, split_axis=0, concat_axis=0, tiled=True)  15 us
    pallas_call x1, Pallas kernels, interpolate(): pl.pallas_call(functools.partial(interp_kernel, elem_count=elem_count), g...  13.2 us
    all_to_all x1, waiting for transfers between devices, local(): lax.all_to_all(answers, axes, split_axis=0, concat_axis=0, tiled=True)  12.6 us
    pallas_call x1, Pallas kernels, place(): pl.pallas_call(functools.partial(place_kernel, peers=peers, width=width,...  11.6 us
    pallas_call x1, Pallas kernels, pick(): pl.pallas_call(pick_kernel, grid=(rows // rows_step,), in_specs=[pl.Block...  9.96 us
    all_to_all x1, starting transfers between devices, local(): lax.all_to_all(placed, axes, split_axis=0, concat_axis=0, tiled=True)  7.32 us
    ppermute x1, waiting for transfers between devices, local(): before = lax.ppermute(departed, axes, [(i, i + 1) for i in range(ends)])  7.07 us
    unnamed x14, local copies, waits for them, and re-layouts  3.26 us
  transfers between devices with their start and end apart: 4, of which 4 were waited for; matrix products, arithmetic and copies ran while one was open for 2% of the time, Pallas kernels for 0%

profile of v2, /device:TPU:0, one launch (start us, length us, event | category | flops | bytes accessed | tf_op | source)
XLA Modules:
  0.0 93.4 jit_solution(303763571207496689)
XLA Ops:
  0.0 11.6 %shard_map.55 = (f32[32,8,512]{2,1,0:T(8,128)}, s32[32,512]{1,0:T(8,128)}) custom-call(f32[3,16384]{1,0:T(4,128)} %depart.1, s32[128,128]{1,0:T(8,128)} %bitcast.10, s32[128,128]{1,0:T(8,128)} %bitcast.11), custom_call_target="tpu_custom_call" | custom-call | tf_op jit(solution)/shard_map/pallas_call | solution.py:109
  11.6 0.0 copy-start.4
  11.6 7.3 %all-to-all-start = ((f32[32,8,512]{2,1,0:T(8,128)}), f32[32,8,512]{2,1,0:T(8,128)S(1)}, u32[]{:S(2)}, u32[]{:S(2)}) async-start(f32[32,8,512]{2,1,0:T(8,128)} %get-tuple-element.7), calls=%async_computation | async-start | bytes 1048576 | tf_op jit(solution)/shard_map/all_to_all | solution.py:305
  18.9 0.0 copy-done.4
  18.9 0.3 copy.9
  19.2 0.9 reshape.16.table
  20.1 15.0 %all-to-all-done.received = f32[32,8,512]{2,1,0:T(8,128)S(1)} async-done(((f32[32,8,512]{2,1,0:T(8,128)}), f32[32,8,512]{2,1,0:T(8,128)S(1)}, u32[]{:S(2)}, u32[]{:S(2)}) %all-to-all-start) | async-done | bytes 524320 | tf_op jit(solution)/shard_map/all_to_all | solution.py:305
  35.2 0.8 copy-done
  36.0 13.2 %shard_map.56 = f32[32,24,128]{2,1,0:T(8,128)} custom-call(f32[32,8,512]{2,1,0:T(8,128)} %copy-done, f32[192,256]{1,0:T(8,128)} %reshape.16.table), custom_call_target="tpu_custom_call" | custom-call | tf_op jit(solution)/shard_map/pallas_call | solution.py:175
  49.2 2.6 %all-to-all-start.1 = ((f32[32,24,128]{2,1,0:T(8,128)}), f32[32,24,128]{2,1,0:T(8,128)S(1)}, u32[]{:S(2)}, u32[]{:S(2)}) async-start(f32[32,24,128]{2,1,0:T(8,128)} %shard_map.56), calls=%async_computation.1 | async-start | bytes 786432 | tf_op jit(solution)/shard_map/all_to_all | solution.py:307
  51.8 0.0 copy-start.5
  51.8 0.7 copy-done.5
  52.5 0.1 copy.12
  52.6 12.6 %all-to-all-done.1.answers = f32[32,24,128]{2,1,0:T(8,128)S(1)} async-done(((f32[32,24,128]{2,1,0:T(8,128)}), f32[32,24,128]{2,1,0:T(8,128)S(1)}, u32[]{:S(2)}, u32[]{:S(2)}) %all-to-all-start.1) | async-done | bytes 393248 | tf_op jit(solution)/shard_map/all_to_all | solution.py:307
  65.2 0.7 copy-done.1
  66.0 10.0 %shard_map.57.own = f32[3,32,512]{2,1,0:T(8,128)} custom-call(f32[32,24,128]{2,1,0:T(8,128)} %copy-done.1, s32[32,512]{1,0:T(8,128)} %get-tuple-element.8.spots), custom_call_target="tpu_custom_call" | custom-call | tf_op jit(solution)/shard_map/pallas_call | solution.py:232
  75.9 2.9 %collective-permute-start = (f32[3,32,512]{2,1,0:T(8,128)}, f32[3,32,512]{2,1,0:T(8,128)S(1)}, u32[]{:S(2)}, u32[]{:S(2)}) collective-permute-start(f32[3,32,512]{2,1,0:T(8,128)} %shard_map.57.own), channel_id=1, source_target_pairs={{0,1},{1,2},{2,3},{3,4},{4,5},{5,6},{6,7},{7,8},{8,9},{9,10},{10,1... | collective-permute-start | bytes 589832 | tf_op jit(solution)/shard_map/ppermute | solution.py:310
  78.8 1.3 %collective-permute-start.1 = (f32[3,32,512]{2,1,0:T(8,128)}, f32[3,32,512]{2,1,0:T(8,128)S(1)}, u32[]{:S(2)}, u32[]{:S(2)}) collective-permute-start(f32[3,32,512]{2,1,0:T(8,128)} %shard_map.57.own), channel_id=1, source_target_pairs={{1,0},{2,1},{3,2},{4,3},{5,4},{6,5},{7,6},{8,7},{9,8},{10,9},{11,1... | collective-permute-start | bytes 589832 | tf_op jit(solution)/shard_map/ppermute | solution.py:311
  80.1 0.6 select_bitcast_fusion.across
  80.7 7.1 %collective-permute-done.before = f32[3,32,512]{2,1,0:T(8,128)S(1)} collective-permute-done((f32[3,32,512]{2,1,0:T(8,128)}, f32[3,32,512]{2,1,0:T(8,128)S(1)}, u32[]{:S(2)}, u32[]{:S(2)}) %collective-permute-start) | collective-permute-done | bytes 196640 | tf_op jit(solution)/shard_map/ppermute | solution.py:310
  87.8 1.9 %collective-permute-done.1.after = f32[3,32,512]{2,1,0:T(8,128)S(1)} collective-permute-done((f32[3,32,512]{2,1,0:T(8,128)}, f32[3,32,512]{2,1,0:T(8,128)S(1)}, u32[]{:S(2)}, u32[]{:S(2)}) %collective-permute-start.1) | collective-permute-done | bytes 196640 | tf_op jit(solution)/shard_map/ppermute | solution.py:311
  89.7 0.0 copy-done.2
  89.7 0.7 copy-done.3
  90.3 3.1 %shard_map.58 = f32[3,32,512]{2,1,0:T(8,128)} custom-call(f32[3,32,512]{2,1,0:T(8,128)} %shard_map.57.own, f32[3,32,512]{2,1,0:T(8,128)} %copy-done.2, f32[3,32,512]{2,1,0:T(8,128)} %copy-done.3, s32[32,6]{1,0:T(8,128)} %select_bitcast_fusion.across), custom_call_target="tpu_custom_call" | custom-call | tf_op jit(solution)/shard_map/pallas_call | solution.py:280
  (4 shorter events, 0.0 us)
Async XLA Ops:
  11.6 7.3 %copy-start.4 = (f32[3,32,512]{2,1,0:T(8,128)S(1)}, f32[3,32,512]{2,1,0:T(8,128)}, u32[]{:S(2)}) copy-start(f32[3,32,512]{2,1,0:T(8,128)} %param.5) | copy-start | bytes 589828
  11.6 23.6 %all-to-all-start = ((f32[32,8,512]{2,1,0:T(8,128)}), f32[32,8,512]{2,1,0:T(8,128)S(1)}, u32[]{:S(2)}, u32[]{:S(2)}) async-start(f32[32,8,512]{2,1,0:T(8,128)} %get-tuple-element.7), calls=%async_computation | async-start | bytes 1048576 | tf_op jit(solution)/shard_map/all_to_all | solution.py:305
  35.2 0.8 copy-start
  49.2 16.0 %all-to-all-start.1 = ((f32[32,24,128]{2,1,0:T(8,128)}), f32[32,24,128]{2,1,0:T(8,128)S(1)}, u32[]{:S(2)}, u32[]{:S(2)}) async-start(f32[32,24,128]{2,1,0:T(8,128)} %shard_map.56), calls=%async_computation.1 | async-start | bytes 786432 | tf_op jit(solution)/shard_map/all_to_all | solution.py:307
  51.8 0.7 copy-start.5
  65.2 0.7 copy-start.1
  75.9 11.9 %collective-permute-start = (f32[3,32,512]{2,1,0:T(8,128)}, f32[3,32,512]{2,1,0:T(8,128)S(1)}, u32[]{:S(2)}, u32[]{:S(2)}) collective-permute-start(f32[3,32,512]{2,1,0:T(8,128)} %shard_map.57.own), channel_id=1, source_target_pairs={{0,1},{1,2},{2,3},{3,4},{4,5},{5,6},{6,7},{7,8},{8,9},{9,10},{10,1... | collective-permute-start | bytes 589832 | tf_op jit(solution)/shard_map/ppermute | solution.py:310
  78.8 10.8 %collective-permute-start.1 = (f32[3,32,512]{2,1,0:T(8,128)}, f32[3,32,512]{2,1,0:T(8,128)S(1)}, u32[]{:S(2)}, u32[]{:S(2)}) collective-permute-start(f32[3,32,512]{2,1,0:T(8,128)} %shard_map.57.own), channel_id=1, source_target_pairs={{1,0},{2,1},{3,2},{4,3},{5,4},{6,5},{7,6},{8,7},{9,8},{10,9},{11,1... | collective-permute-start | bytes 589832 | tf_op jit(solution)/shard_map/ppermute | solution.py:311
  87.8 1.9 %copy-start.2 = (f32[3,32,512]{2,1,0:T(8,128)}, f32[3,32,512]{2,1,0:T(8,128)S(1)}, u32[]{:S(2)}) copy-start(f32[3,32,512]{2,1,0:T(8,128)S(1)} %collective-permute-done.before) | copy-start | bytes 589828
  89.7 0.7 copy-start.3
